TPU v7x, 32 devices: a whole 2x2x4 slice. The times are simulated.
32 devices in a mesh: dp: 8 (over z, y), tensor: 4 (over x, core).
Axes of the slice: x: 2, y: 2, z: 4, core: 2. Of those that a mesh axis runs over, the one named last changes fastest.
Arguments:
- image_rows: bfloat16 [16, 197, 768], P('dp', None, 'tensor'), may hold values from -6 to 6
- text_rows: bfloat16 [8, 512, 768], P('dp', None, 'tensor'), may hold values from -6 to 6
- pair_rows: bfloat16 [8, 711, 768], P('dp', None, 'tensor'), may hold values from -6 to 6
- text_lengths: int32 [8], P('dp'), may hold values from 128 to 512, as said below
- pair_lengths: int32 [8], P('dp'), may hold values from 128 to 512, as said below
- qkv_weight: bfloat16 [3, 768, 3, 768], P(None, None, None, 'tensor'), may hold values from -0.21875 to 0.21875
- qv_bias: bfloat16 [3, 2, 768], P(None, None, 'tensor'), may hold values from -3 to 3
- out_weight: bfloat16 [3, 768, 768], P(None, 'tensor'), may hold values from -3.5 to 3.5
- out_bias: bfloat16 [3, 768], P(None, 'tensor'), may hold values from -3 to 3
- up_weight: bfloat16 [3, 768, 3072], P(None, None, 'tensor'), may hold values from -0.21875 to 0.21875
- up_bias: bfloat16 [3, 3072], P(None, 'tensor'), may hold values from -3 to 3
- down_weight: bfloat16 [3, 3072, 768], P(None, 'tensor'), may hold values from -0.109375 to 0.109375
- down_bias: bfloat16 [3, 768], P(None, 'tensor'), may hold values from -3 to 3
- norm_gain: bfloat16 [3, 2, 768], P(None, None, 'tensor'), may hold values from 0.099609375 to 1.8984375
- norm_bias: bfloat16 [3, 2, 768], P(None, None, 'tensor'), may hold values from -3 to 3
- image_upstream: bfloat16 [16, 197, 768], P('dp', None, 'tensor'), may hold values from -6 to 6
- text_upstream: bfloat16 [8, 512, 768], P('dp', None, 'tensor'), may hold values from -6 to 6
- pair_upstream: bfloat16 [8, 711, 768], P('dp', None, 'tensor'), may hold values from -6 to 6
Outputs:
- image_out: bfloat16 [16, 197, 768], P('dp', None, 'tensor')
- text_out: bfloat16 [8, 512, 768], P('dp', None, 'tensor')
- pair_out: bfloat16 [8, 711, 768], P('dp', None, 'tensor')
- image_input_grad: bfloat16 [16, 197, 768], P('dp', None, 'tensor')
- text_input_grad: bfloat16 [8, 512, 768], P('dp', None, 'tensor')
- pair_input_grad: bfloat16 [8, 711, 768], P('dp', None, 'tensor')
- qkv_grad: float32 [3, 768, 3, 768], P(None, 'dp', None, 'tensor')
- qv_bias_grad: float32 [3, 2, 768], P(None, None, 'tensor')
- out_weight_grad: float32 [3, 768, 768], P(None, 'tensor', 'dp')
- out_bias_grad: float32 [3, 768], P(None, 'tensor')
- up_weight_grad: float32 [3, 768, 3072], P(None, 'dp', 'tensor')
- up_bias_grad: float32 [3, 3072], P(None, 'tensor')
- down_weight_grad: float32 [3, 3072, 768], P(None, 'tensor', 'dp')
- down_bias_grad: float32 [3, 768], P(None, 'tensor')
- norm_gain_grad: float32 [3, 2, 768], P(None, None, 'tensor')
- norm_bias_grad: float32 [3, 2, 768], P(None, None, 'tensor')
Inputs may be any that keep to these rules, and one draw needn't show every extreme that they name: Each text example's first text_lengths rows of 512 are valid; some example of every draw has all 512. Each pair's text rows after its 197 image rows: the first pair_lengths are valid, the rest and the two pad rows are not; some pair of every draw has all 512.
All inputs are finite; a program needn't handle non-finite values.
Results may differ from a plain program's by a relative error of at most 0.017.
Values may be sent and summed in bfloat16 or wider, within the bound.
A program may use at most 192 MiB of HBM per device.

v0:
```python
import math
import jax
import jax.numpy as jnp
from jax import lax
from jax.sharding import PartitionSpec as P

HEAD_DIM = 64
PATCHES = 196
EPSILON = 1e-06


def rounded(value):
    return lax.optimization_barrier(value.astype(jnp.bfloat16)).astype(jnp.float32)


def moments(total_count, square, feature_width):
    mean_val = total_count / feature_width
    return (mean_val, lax.rsqrt(square / feature_width - mean_val * mean_val + EPSILON))


def local_moments(value, feature_width):
    return moments(
        jnp.sum(value, axis=-1, keepdims=True),
        jnp.sum(value * value, axis=-1, keepdims=True),
        feature_width,
    )


def gather_grads(value):
    return lax.all_gather(value, "tensor", axis=2, tiled=True)


def summed_grads(value):
    return lax.psum_scatter(
        rounded(value).astype(jnp.bfloat16), "tensor", scatter_dimension=2, tiled=True
    ).astype(jnp.float32)


def norm_reverse_pass(centered_grad, standardized, inverse_deviation, feature_width):
    total_count, cross_term = lax.psum(
        (
            jnp.sum(centered_grad, axis=-1, keepdims=True),
            jnp.sum(centered_grad * standardized, axis=-1, keepdims=True),
        ),
        "tensor",
    )
    return inverse_deviation * (
        centered_grad - total_count / feature_width - standardized * cross_term / feature_width
    )


def gelu_exact(value):
    return jax.nn.gelu(value, approximate=False)


def masked_scores(queries, key_heads, key_mask, scale):
    scores = (
        jnp.einsum("elhd,emhd->ehlm", queries, key_heads, preferred_element_type=jnp.float32)
        * scale
    )
    return jnp.where(key_mask[:, None, None, :], scores, -1000000000.0)


def forward_tower(row_block, key_mask, weights, tensor_index):
    qkv_w, qv_b, out_w, out_b, up_w, up_b, down_w, down_b, gain, shift = weights
    feature_width = qkv_w.shape[0]
    share = out_w.shape[0]
    examples = row_block.shape[0]
    length = row_block.shape[1]
    head_count = share // HEAD_DIM
    scale = 1.0 / math.sqrt(HEAD_DIM)
    rows_float = row_block.astype(jnp.float32)
    whole_rows, whole_bias, whole_gain, whole_shift = (
        lax.all_gather(row_block, "tensor", axis=2, tiled=True),
        lax.all_gather(out_b, "tensor", axis=0, tiled=True),
        lax.all_gather(gain, "tensor", axis=1, tiled=True),
        lax.all_gather(shift, "tensor", axis=1, tiled=True),
    )
    whole_f = whole_rows.astype(jnp.float32)
    input_mean, input_inverse_deviation = local_moments(whole_f, feature_width)
    normed = (
        (whole_f - input_mean) * input_inverse_deviation * whole_gain[0].astype(jnp.float32)
        + whole_shift[0].astype(jnp.float32)
    ).astype(jnp.bfloat16)
    projected = jnp.einsum("eld,dcf->elcf", normed, qkv_w, preferred_element_type=jnp.float32)
    queries = (
        (projected[:, :, 0] + qv_b[0].astype(jnp.float32))
        .astype(jnp.bfloat16)
        .reshape(examples, length, head_count, HEAD_DIM)
    )
    key_heads = (
        projected[:, :, 1].astype(jnp.bfloat16).reshape(examples, length, head_count, HEAD_DIM)
    )
    value_heads = (
        (projected[:, :, 2] + qv_b[1].astype(jnp.float32))
        .astype(jnp.bfloat16)
        .reshape(examples, length, head_count, HEAD_DIM)
    )
    scores = masked_scores(queries, key_heads, key_mask, scale)
    top_score = jnp.max(scores, axis=-1, keepdims=True)
    log_total = top_score + jnp.log(jnp.sum(jnp.exp(scores - top_score), axis=-1, keepdims=True))
    probs_low = jnp.exp(scores - log_total).astype(jnp.bfloat16)
    mixed = (
        jnp.einsum("ehlm,emhd->elhd", probs_low, value_heads, preferred_element_type=jnp.float32)
        .astype(jnp.bfloat16)
        .reshape(examples, length, share)
    )
    partial_value = jnp.einsum("elf,fd->eld", mixed, out_w, preferred_element_type=jnp.float32)
    attn_full = lax.psum(rounded(partial_value).astype(jnp.bfloat16), "tensor").astype(
        jnp.float32
    ) + whole_bias.astype(jnp.float32)
    resid_full = whole_f + attn_full
    middle_mean, middle_inverse_deviation = local_moments(resid_full, feature_width)
    normed_two = (
        (resid_full - middle_mean) * middle_inverse_deviation * whole_gain[1].astype(jnp.float32)
        + whole_shift[1].astype(jnp.float32)
    ).astype(jnp.bfloat16)
    attention = lax.dynamic_slice_in_dim(attn_full, tensor_index * share, share, 2)
    residual_stream = rows_float + attention
    hidden = jnp.einsum(
        "eld,df->elf", normed_two, up_w, preferred_element_type=jnp.float32
    ) + up_b.astype(jnp.float32)
    activated = gelu_exact(hidden).astype(jnp.bfloat16)
    down_part = jnp.einsum("elf,fd->eld", activated, down_w, preferred_element_type=jnp.float32)
    feedforward = lax.psum_scatter(
        rounded(down_part).astype(jnp.bfloat16), "tensor", scatter_dimension=2, tiled=True
    ).astype(jnp.float32) + down_b.astype(jnp.float32)
    output = residual_stream + feedforward
    kept = (
        normed,
        queries,
        key_heads,
        value_heads,
        log_total,
        mixed,
        normed_two,
        hidden,
        activated,
        input_mean,
        input_inverse_deviation,
        middle_mean,
        middle_inverse_deviation,
        residual_stream,
        rows_float,
    )
    return (output, kept)


def backward_tower(upstream, weights, kept, key_mask):
    qkv_w, qv_b, out_w, out_b, up_w, up_b, down_w, down_b, gain, shift = weights
    (
        normed,
        queries,
        key_heads,
        value_heads,
        log_total,
        mixed,
        normed_two,
        hidden,
        activated,
        input_mean,
        input_inverse_deviation,
        middle_mean,
        middle_inverse_deviation,
        residual_stream,
        rows_float,
    ) = kept
    feature_width = qkv_w.shape[0]
    share = out_w.shape[0]
    examples = queries.shape[0]
    length = queries.shape[1]
    head_count = share // HEAD_DIM
    scale = 1.0 / math.sqrt(HEAD_DIM)
    gain_float = gain.astype(jnp.float32)
    output_gradient = upstream.astype(jnp.float32)
    grad_ffn = output_gradient.astype(jnp.bfloat16)
    down_bias_grad = jnp.sum(grad_ffn, axis=(0, 1), dtype=jnp.float32)
    ffn_full = gather_grads(grad_ffn)
    down_grad = jnp.einsum("elf,eld->fd", activated, ffn_full, preferred_element_type=jnp.float32)
    grad_act = jnp.einsum("eld,fd->elf", ffn_full, down_w, preferred_element_type=jnp.float32)
    grad_hidden = jax.vjp(gelu_exact, hidden)[1](grad_act)[0].astype(jnp.bfloat16)
    up_bias_grad = jnp.sum(grad_hidden, axis=(0, 1), dtype=jnp.float32)
    up_grad = jnp.einsum("eld,elf->df", normed_two, grad_hidden, preferred_element_type=jnp.float32)
    second_normed_gradient = summed_grads(
        jnp.einsum("elf,df->eld", grad_hidden, up_w, preferred_element_type=jnp.float32)
    )
    standardized_middle = (residual_stream - middle_mean) * middle_inverse_deviation
    middle_gain_grad = jnp.sum(second_normed_gradient * standardized_middle, axis=(0, 1))
    shift_mid_grad = jnp.sum(second_normed_gradient, axis=(0, 1))
    residual_gradient = output_gradient + norm_reverse_pass(
        second_normed_gradient * gain_float[1],
        standardized_middle,
        middle_inverse_deviation,
        feature_width,
    )
    grad_attn = residual_gradient.astype(jnp.bfloat16)
    out_bias_grad = jnp.sum(grad_attn, axis=(0, 1), dtype=jnp.float32)
    attn_full = gather_grads(grad_attn)
    out_grad = jnp.einsum("elf,eld->fd", mixed, attn_full, preferred_element_type=jnp.float32)
    grad_mixed = (
        jnp.einsum("eld,fd->elf", attn_full, out_w, preferred_element_type=jnp.float32)
        .astype(jnp.bfloat16)
        .reshape(examples, length, head_count, HEAD_DIM)
    )
    scores = masked_scores(queries, key_heads, key_mask, scale)
    probs_f = jnp.exp(scores - log_total)
    probs_low = probs_f.astype(jnp.bfloat16)
    grad_values = jnp.einsum(
        "ehlm,elhd->emhd", probs_low, grad_mixed, preferred_element_type=jnp.float32
    ).astype(jnp.bfloat16)
    grad_probs = jnp.einsum(
        "elhd,emhd->ehlm", grad_mixed, value_heads, preferred_element_type=jnp.float32
    )
    grad_scores = (
        probs_f * (grad_probs - jnp.sum(probs_f * grad_probs, axis=-1, keepdims=True))
    ).astype(jnp.bfloat16)
    grad_queries = (
        jnp.einsum("ehlm,emhd->elhd", grad_scores, key_heads, preferred_element_type=jnp.float32)
        * scale
    ).astype(jnp.bfloat16)
    grad_keys = (
        jnp.einsum("ehlm,elhd->emhd", grad_scores, queries, preferred_element_type=jnp.float32)
        * scale
    ).astype(jnp.bfloat16)
    grad_qkv = jnp.stack([grad_queries, grad_keys, grad_values], 2).reshape(
        examples, length, 3, share
    )
    qv_bias_grad = jnp.stack(
        [
            jnp.sum(grad_qkv[:, :, 0], axis=(0, 1), dtype=jnp.float32),
            jnp.sum(grad_qkv[:, :, 2], axis=(0, 1), dtype=jnp.float32),
        ],
        0,
    )
    qkv_grad = jnp.einsum("eld,elcf->dcf", normed, grad_qkv, preferred_element_type=jnp.float32)
    normed_gradient = summed_grads(
        jnp.einsum("elcf,dcf->eld", grad_qkv, qkv_w, preferred_element_type=jnp.float32)
    )
    standardized_input = (rows_float - input_mean) * input_inverse_deviation
    input_gain_grad = jnp.sum(normed_gradient * standardized_input, axis=(0, 1))
    shift_in_grad = jnp.sum(normed_gradient, axis=(0, 1))
    grad_input = (
        residual_gradient
        + norm_reverse_pass(
            normed_gradient * gain_float[0],
            standardized_input,
            input_inverse_deviation,
            feature_width,
        )
    ).astype(jnp.bfloat16)
    small_grads = jnp.concatenate(
        [
            qv_bias_grad,
            out_bias_grad[None],
            up_bias_grad.reshape(-1, share),
            down_bias_grad[None],
            jnp.stack([input_gain_grad, middle_gain_grad], 0),
            jnp.stack([shift_in_grad, shift_mid_grad], 0),
        ],
        0,
    )
    return (grad_input, (qkv_grad, out_grad, up_grad, down_grad, small_grads))


def per_device(
    image_rows,
    text_rows,
    pair_rows,
    text_lengths,
    pair_lengths,
    qkv_weight,
    qv_bias,
    out_weight,
    out_bias,
    up_weight,
    up_bias,
    down_weight,
    down_bias,
    norm_gain,
    norm_bias,
    image_upstream,
    text_upstream,
    pair_upstream,
):
    tensor_index = lax.axis_index("tensor")
    image_mask = jnp.ones((image_rows.shape[0], image_rows.shape[1]), dtype=bool)
    text_mask = jnp.arange(text_rows.shape[1], dtype=jnp.int32)[None, :] < text_lengths[:, None]
    pair_mask = jnp.arange(pair_rows.shape[1], dtype=jnp.int32)[None, :] < pair_lengths[:, None] + (
        PATCHES + 1
    )
    towers_in = (
        (image_rows, image_mask, image_upstream),
        (text_rows, text_mask, text_upstream),
        (pair_rows, pair_mask, pair_upstream),
    )
    params = (
        qkv_weight,
        qv_bias,
        out_weight,
        out_bias,
        up_weight,
        up_bias,
        down_weight,
        down_bias,
        norm_gain,
        norm_bias,
    )
    outputs = []
    input_grads = []
    grad_lists = ([], [], [], [], [])
    for tower_id in range(3):
        row_block, key_mask, upstream = towers_in[tower_id]
        weights = tuple((entry[tower_id] for entry in params))
        output, kept = forward_tower(row_block, key_mask, weights, tensor_index)
        outputs.append(output.astype(jnp.bfloat16))
        grad_input, grads = backward_tower(upstream, weights, kept, key_mask)
        input_grads.append(grad_input)
        for slot_id in range(5):
            grad_lists[slot_id].append(grads[slot_id])
    stacked = tuple((jnp.stack(group_list, 0) for group_list in grad_lists))
    qkv_grad, out_weight_grad, up_weight_grad, down_weight_grad = (
        lax.psum_scatter(stacked[0], "dp", scatter_dimension=1, tiled=True),
        lax.psum_scatter(stacked[1], "dp", scatter_dimension=2, tiled=True),
        lax.psum_scatter(stacked[2], "dp", scatter_dimension=1, tiled=True),
        lax.psum_scatter(stacked[3], "dp", scatter_dimension=2, tiled=True),
    )
    small_grads = lax.psum(stacked[4], "dp")
    share = out_weight.shape[1]
    hidden_share = up_weight.shape[2]
    ratio = hidden_share // share
    qv_bias_grad = small_grads[:, 0:2]
    out_bias_grad = small_grads[:, 2]
    up_bias_grad = small_grads[:, 3 : 3 + ratio].reshape(3, hidden_share)
    down_bias_grad = small_grads[:, 3 + ratio]
    norm_gain_grad = small_grads[:, 4 + ratio : 6 + ratio]
    norm_bias_grad = small_grads[:, 6 + ratio : 8 + ratio]
    return (
        outputs[0],
        outputs[1],
        outputs[2],
        input_grads[0],
        input_grads[1],
        input_grads[2],
        qkv_grad,
        qv_bias_grad,
        out_weight_grad,
        out_bias_grad,
        up_weight_grad,
        up_bias_grad,
        down_weight_grad,
        down_bias_grad,
        norm_gain_grad,
        norm_bias_grad,
    )


def solution(mesh):
    return jax.shard_map(
        per_device,
        mesh=mesh,
        in_specs=(
            P("dp", None, "tensor"),
            P("dp", None, "tensor"),
            P("dp", None, "tensor"),
            P("dp"),
            P("dp"),
            P(None, None, None, "tensor"),
            P(None, None, "tensor"),
            P(None, "tensor", None),
            P(None, "tensor"),
            P(None, None, "tensor"),
            P(None, "tensor"),
            P(None, "tensor", None),
            P(None, "tensor"),
            P(None, None, "tensor"),
            P(None, None, "tensor"),
            P("dp", None, "tensor"),
            P("dp", None, "tensor"),
            P("dp", None, "tensor"),
        ),
        out_specs=(
            P("dp", None, "tensor"),
            P("dp", None, "tensor"),
            P("dp", None, "tensor"),
            P("dp", None, "tensor"),
            P("dp", None, "tensor"),
            P("dp", None, "tensor"),
            P(None, "dp", None, "tensor"),
            P(None, None, "tensor"),
            P(None, "tensor", "dp"),
            P(None, "tensor"),
            P(None, "dp", "tensor"),
            P(None, "tensor"),
            P(None, "tensor", "dp"),
            P(None, "tensor"),
            P(None, None, "tensor"),
            P(None, None, "tensor"),
        ),
        check_vma=False,
    )
```

profile of v0, /device:TPU:0, one launch (start us, length us, event | category | flops | bytes accessed | tf_op | source)
XLA Modules:
  0.0 1013.4 jit_solution(11684703509112066378)
XLA Ops:
  8.7 7.9 all-gather.1
  35.5 8.7 all_gather.54
  56.0 12.3 %all_gather.58 = bf16[1,512,768]{1,2,0:T(8,128)(2,1)S(1)} all-gather(bf16[1,512,192]{1,2,0:T(8,128)(2,1)S(1)} %copy-done.81), channel_id=1, replica_groups=mesh['dp'=8,'tensor'=4] {'tensor'}, dimensions={2}, use_global_device_ids=true | all-gather | bytes 983040 | tf_op jit(solution)/shard_map/all_gather | solution.py:74
  68.7 6.6 all-gather.4
  80.8 8.5 all-gather.3
  100.1 8.3 all-reduce.8
  145.3 9.7 all_gather.66
  192.1 10.5 %all_gather.68 = bf16[1,512,768]{1,2,0:T(8,128)(2,1)} all-gather(bf16[1,512,192]{1,2,0:T(8,128)(2,1)S(1)} %copy-done.82), channel_id=1, replica_groups=mesh['dp'=8,'tensor'=4] {'tensor'}, dimensions={2}, use_global_device_ids=true | all-gather | bytes 983040 | tf_op jit(solution)/shard_map/all_gather | solution.py:30
  202.6 51.6 %all-reduce.19.cloned.1.call-done = (bf16[1,512,768]{2,1,0:T(8,128)(2,1)}, bf16[1,711,768]{2,1,0:T(8,128)(2,1)}, bf16[2,197,768]{1,0,2:T(2,128)(2,1)}) async-done(((bf16[1,512,768]{2,1,0:T(8,128)(2,1)}, bf16[1,711,768]{2,1,0:T(8,128)(2,1)}, bf16[2,197,768]{1,0,2:T(2,128)(2,1)}), (bf16[1,512,768]{2,1,0:T(8,128)(2,1)}, bf16[1,711,768]{2,1,0:T(8,128)(2,1)}, ...) | async-done | bytes 2483728 | tf_op jit(solution)/shard_map/psum | solution.py:109
  290.5 9.1 multiply_convert_fusion.2
  309.3 6.7 copy.229
  359.6 6.7 copy.223
  389.0 11.6 %all-reduce.7 = (f32[2,197]{1,0:T(2,128)}, f32[2,197,1]{1,0,2:T(2,128)}, f32[512]{0:T(512)}, f32[1,512,1]{1,2,0:T(1,128)}, f32[711]{0:T(1024)}, /*index=5*/f32[1,711,1]{1,2,0:T(1,128)}) all-reduce(f32[2,197]{1,0:T(2,128)} %get-tuple-element.87, f32[2,197,1]{1,0,2:T(2,128)} %bitcast.503, ...), channel_id=1, replica_groups=mesh['dp'=8,'tensor'=4] {'tensor'}, use_global_device_ids=true, to_apply=%region_28.29 | all-reduce | flops 3234 | bytes 25872 | tf_op jit(solution)/shard_map/psum | solution.py:40
  406.0 9.1 all_gather.67
  443.5 9.0 all_gather.69
  507.6 11.0 %copy.237 = f32[3,768,768]{1,0,2:T(4,128)} copy(f32[3,768,768]{2,1,0:T(8,128)} %pad_maximum_fusion.1) | data formatting | bytes 14155776
  518.5 8.2 copy.255
  535.6 9.8 copy.233
  545.4 11.3 %reshape.1241 = f32[768,1728]{1,0:T(8,128)} reshape(f32[768,3,3,192]{3,2,1,0:T(4,128)} %bitcast.422) | data formatting | bytes 10616832
  577.5 10.9 %all-reduce.6 = (f32[2,197]{1,0:T(2,128)S(1)}, f32[2,197,1]{1,0,2:T(2,128)S(1)}, f32[512]{0:T(512)S(1)}, f32[1,512,1]{1,2,0:T(1,128)S(1)}, f32[711]{0:T(1024)S(1)}, /*index=5*/f32[1,711,1]{1,2,0:T(1,128)S(1)}) all-reduce(f32[2,197]{1,0:T(2,128)S(1)} %get-tuple-element.105, ...), channel_id=1, replica_groups=mesh['dp'=8,'tensor'=4] {'tensor'}, use_global_device_ids=true, to_apply=%region_34.35 | all-reduce | flops 3234 | bytes 25872 | tf_op jit(solution)/shard_map/psum | solution.py:40
  597.3 38.3 %psum.127 = f32[3,12,192]{2,1,0:T(8,128)S(1)} all-reduce(f32[3,12,192]{2,1,0:T(8,128)S(1)} %pad_maximum_fusion.9), channel_id=1, replica_groups=mesh['dp'=8,'tensor'=4] {'dp'}, use_global_device_ids=true, to_apply=%region_85.86 | all-reduce | flops 6912 | bytes 55296 | tf_op jit(solution)/shard_map/psum | solution.py:327
  639.6 124.9 %reduce-scatter.47.cloned.1.call-done = f32[96,2304]{1,0:T(8,128)} async-done(((f32[768,2304]{1,0:T(8,128)}), f32[96,2304]{1,0:T(8,128)}) %reduce-scatter.47.cloned.1.call-update) | async-done | bytes 884752
  767.2 106.9 %reduce-scatter.43.cloned.1.call-done = f32[96,1728]{1,0:T(8,128)} async-done(((f32[768,1728]{1,0:T(8,128)}), f32[96,1728]{1,0:T(8,128)}) %reduce-scatter.43.cloned.1.call-update) | async-done | bytes 663568
  876.9 129.8 %reduce-scatter.29.cloned.1.call-done = f32[3,96,768]{2,1,0:T(8,128)} async-done(((f32[3,768,768]{2,1,0:T(8,128)}), f32[3,96,768]{2,1,0:T(8,128)}) %reduce-scatter.29.cloned.1.call-update) | async-done | bytes 884752 | tf_op jit(solution)/shard_map/reduce_scatter | solution.py:324
  (724 shorter events, 366.5 us)
Async XLA Ops:
  7.2 147.8 %all-reduce.15.cloned.1.call-start = ((), (), s32[]{:S(2)}) async-start(), calls=%async_computation.10 | async-start | bytes 1228800 | tf_op jit(solution)/shard_map/psum | solution.py:109
  52.7 120.8 %all-gather.13.cloned.1.call-start = ((), (), s32[]{:S(2)}) async-start(), calls=%async_computation.11 | async-start | bytes 1474560 | tf_op jit(solution)/shard_map/all_gather | solution.py:74
  53.4 200.8 %all-reduce.19.cloned.1.call-start = ((), (), s32[]{:S(2)}) async-start(), calls=%async_computation.25 | async-start | bytes 5332992 | tf_op jit(solution)/shard_map/psum | solution.py:109
  121.8 61.7 %copy-start.110 = (pred[711]{0:T(1024)(128)(4,1)}, pred[711]{0:T(1024)(128)(4,1)S(1)}, u32[]{:S(2)}) copy-start(pred[711]{0:T(1024)(128)(4,1)S(1)} %iota_compare_fusion) | copy-start | bytes 2137
  133.5 44.0 %copy-start.182 = (f32[768]{0:T(1024)}, f32[768]{0:T(1024)S(1)}, u32[]{:S(2)}) copy-start(f32[768]{0:T(1024)S(1)} %get-tuple-element.108) | copy-start | bytes 9220
  133.5 156.9 %copy-start.178 = (f32[768]{0:T(1024)}, f32[768]{0:T(1024)S(1)}, u32[]{:S(2)}) copy-start(f32[768]{0:T(1024)S(1)} %get-tuple-element.109) | copy-start | bytes 9220
  145.1 145.4 %copy-start.180 = (f32[768]{0:T(1024)}, f32[768]{0:T(1024)S(1)}, u32[]{:S(2)}) copy-start(f32[768]{0:T(1024)S(1)} %get-tuple-element.107) | copy-start | bytes 9220
  145.2 35.2 %copy-start.134 = (f32[3,64]{1,0:T(4,128)}, f32[3,64]{1,0:T(4,128)S(1)}, u32[]{:S(2)}) copy-start(f32[3,64]{1,0:T(4,128)S(1)} %reshape.1120) | copy-start | bytes 2308
  145.2 41.0 %copy-start.136 = (f32[3,64]{1,0:T(4,128)}, f32[3,64]{1,0:T(4,128)S(1)}, u32[]{:S(2)}) copy-start(f32[3,64]{1,0:T(4,128)S(1)} %reshape.1119) | copy-start | bytes 2308
  191.2 108.4 %all-gather.15.cloned.1.call-start = ((), (), s32[]{:S(2)}) async-start(), calls=%async_computation.12 | async-start | bytes 1474560 | tf_op jit(solution)/shard_map/all_gather | solution.py:30
  191.8 179.9 %reduce-scatter.35.cloned.1.call-start = ((), (), s32[]{:S(2)}) async-start(), calls=%async_computation.17 | async-start | bytes 983040
  192.1 65.1 %copy-start.142 = (f32[768]{0:T(1024)}, f32[768]{0:T(1024)S(1)}, u32[]{:S(2)}) copy-start(f32[768]{0:T(1024)S(1)} %convert_element_type.888) | copy-start | bytes 9220
  277.9 97.5 %reduce-scatter.31.cloned.1.call-start = ((), (), s32[]{:S(2)}) async-start(), calls=%async_computation.15 | async-start | bytes 983040
  290.4 91.2 %reduce-scatter.39.cloned.1.call-start = ((), (), s32[]{:S(2)}) async-start(), calls=%async_computation.19 | async-start | bytes 1474560
  318.9 114.5 %reduce-scatter.33.cloned.1.call-start = ((), (), s32[]{:S(2)}) async-start(), calls=%async_computation.16 | async-start | bytes 1474560
  324.6 112.9 %copy-start.9 = (bf16[1,711,192]{2,1,0:T(8,128)(2,1)}, bf16[1,711,192]{2,1,0:T(8,128)(2,1)S(1)}, u32[]{:S(2)}) copy-start(bf16[1,711,192]{2,1,0:T(8,128)(2,1)S(1)} %copy.168) | copy-start | bytes 819076
  369.2 100.9 %all-gather.17.cloned.1.call-start = ((), (), s32[]{:S(2)}) async-start(), calls=%async_computation.13 | async-start | bytes 1474560 | tf_op jit(solution)/shard_map/all_gather | solution.py:30
  443.5 125.9 %all-reduce.17.cloned.1.call-start = ((), (), s32[]{:S(2)}) async-start(), calls=%async_computation.24 | async-start | bytes 3145728
  459.6 112.8 %reduce-scatter.37.cloned.1.call-start = ((), (), s32[]{:S(2)}) async-start(), calls=%async_computation.18 | async-start | bytes 983040
  469.9 104.9 %reduce-scatter.41.cloned.1.call-start = ((), (), s32[]{:S(2)}) async-start(), calls=%async_computation.20 | async-start | bytes 1474560
  489.9 147.6 %reduce-scatter.45.cloned.1.call-start = ((), (), s32[]{:S(2)}) async-start(), calls=%async_computation.22 | async-start | bytes 2211840
  499.4 265.1 %reduce-scatter.47.cloned.1.call-start = ((), (), s32[]{:S(2)}) async-start(), calls=%async_computation.23 | async-start | bytes 7962624
  526.8 347.3 %reduce-scatter.43.cloned.1.call-start = ((), (), s32[]{:S(2)}) async-start(), calls=%async_computation.21 | async-start | bytes 6193152
  556.8 449.9 %reduce-scatter.29.cloned.1.call-start = ((), (), s32[]{:S(2)}) async-start(), calls=%async_computation.14 | async-start | bytes 7962624 | tf_op jit(solution)/shard_map/reduce_scatter | solution.py:324
  (216 other events, 1050.3 us)
Sparse Core Ops, SparseCore 0:
  52.8 36.7 all-reduce.14
  91.1 18.1 all-gather.12
  191.3 62.8 all-reduce.18
  255.6 17.4 all-gather.14
  278.0 23.3 reduce-scatter.34
  303.8 23.2 reduce-scatter.30
  329.6 25.6 reduce-scatter.38
  369.3 25.7 reduce-scatter.32
  443.6 17.4 all-gather.16
  464.5 42.8 all-reduce.16
  509.9 23.2 reduce-scatter.36
  535.6 25.6 reduce-scatter.40
  564.8 67.8 reduce-scatter.44
  636.2 128.2 reduce-scatter.46
  768.0 106.0 reduce-scatter.42
  878.2 128.5 reduce-scatter.28
where the time goes:
time: 1030 us; the launch traced here: 1010 us
  waiting for transfers between devices  415 us (40%)
  local copies, waits for them, and re-layouts  204 us (20%)
  blocking collectives  171 us (17%)
  matrix products  106 us (10%)
  other arithmetic  96.2 us (9%)
  between operations  19.5 us (2%)
    unnamed x26, waiting for transfers between devices  233 us
    unnamed x514, local copies, waits for them, and re-layouts  160 us
    reduce_scatter x1, waiting for transfers between devices, per_device(): lax.psum_scatter(stacked[2], 'dp', scatter_dimension=1, tiled=True)  130 us
    psum x2, waiting for transfers between devices, forward_tower(): lax.psum(rounded(partial_value).astype(jnp.bfloat16), 'tensor')  51.6 us
    all_gather x4, blocking collectives, gather_grads(): return lax.all_gather(value, 'tensor', axis=2, tiled=True)  38.4 us
    psum x1, blocking collectives, per_device(): small_grads = lax.psum(stacked[4], 'dp')  38.3 us
    psum x2, blocking collectives, norm_reverse_pass(): lax.psum((jnp.sum(centered_grad, axis=-1, keepdims=True), jnp.sum(centere...  22.5 us
    all_gather x3, blocking collectives, forward_tower(): lax.all_gather(gain, 'tensor', axis=1, tiled=True)  21.7 us
  transfers between devices with their start and end apart: 16, of which 4 were waited for; matrix products, arithmetic and copies ran while one was open for 34% of the time, Pallas kernels for 0%

commit v1 on v0

--- a/solution.py
+++ b/solution.py
@@ -7,6 +7,18 @@
 HEAD_DIM = 64
 PATCHES = 196
 EPSILON = 1e-06
+
+
+def gather_by_bits(value, axis, dim):
+    ways, here, step = (lax.axis_size(axis), lax.axis_index(axis), value.shape[dim])
+    line, have = (value, 1)
+    while have < ways:
+        line = jnp.concatenate(
+            [line, lax.ppermute(line, axis, [(d, (d - have) % ways) for d in range(ways)])],
+            axis=dim,
+        )
+        have = 2 * have
+    return jnp.roll(line, here * step, axis=dim)
 
 
 def rounded(value):
@@ -73,7 +85,7 @@
     whole_rows, whole_bias, whole_gain, whole_shift = (
         lax.all_gather(row_block, "tensor", axis=2, tiled=True),
         lax.all_gather(out_b, "tensor", axis=0, tiled=True),
-        lax.all_gather(gain, "tensor", axis=1, tiled=True),
+        gather_by_bits(gain, "tensor", 1),
         lax.all_gather(shift, "tensor", axis=1, tiled=True),
     )
     whole_f = whole_rows.astype(jnp.float32)

time: 1030 us -> 980 us (0.951)
  blocking collectives: 171 us -> 152 us
  local copies, waits for them, and re-layouts: 204 us -> 189 us
  other arithmetic: 96.2 us -> 82.5 us
  waiting for transfers between devices: 415 us -> 404 us
    all_gather x3 -> x0, blocking collectives: 21.7 us -> none  [forward_tower(): lax.all_gather(gain, 'tensor', axis=1, tiled=True)]
    convert_element_type x3, other arithmetic: 15.3 us -> 1.84 us  [forward_tower(): whole_gain[0].astype(jnp.float32)]
    unnamed x26, waiting for transfers between devices: 233 us -> 220 us
    slice x3 -> x2, local copies, waits for them, and re-layouts: 13.6 us -> 1.18 us  [backward_tower(): gain_float[0]]
    unnamed x514 -> x488, local copies, waits for them, and re-layouts: 160 us -> 160 us
  transfers between devices with their start and end apart: 16 -> 22, of which waited for: 4 -> 6; matrix products, arithmetic and copies ran while one was open for 34% -> 34% of each run, Pallas kernels for 0% -> 0%
where the time goes in v1:
time: 980 us; the launch traced here: 969 us
  waiting for transfers between devices  404 us (41%)
  local copies, waits for them, and re-layouts  189 us (19%)
  blocking collectives  152 us (16%)
  matrix products  114 us (12%)
  other arithmetic  82.5 us (8%)
  between operations  19.6 us (2%)
    unnamed x26, waiting for transfers between devices  220 us
    unnamed x488, local copies, waits for them, and re-layouts  160 us
    reduce_scatter x1, waiting for transfers between devices, per_device(): lax.psum_scatter(stacked[2], 'dp', scatter_dimension=1, tiled=True)  130 us
    psum x2, waiting for transfers between devices, forward_tower(): lax.psum(rounded(partial_value).astype(jnp.bfloat16), 'tensor')  51 us
    all_gather x4, blocking collectives, gather_grads(): return lax.all_gather(value, 'tensor', axis=2, tiled=True)  41.5 us
    psum x1, blocking collectives, per_device(): small_grads = lax.psum(stacked[4], 'dp')  38.5 us
    psum x2, blocking collectives, norm_reverse_pass(): lax.psum((jnp.sum(centered_grad, axis=-1, keepdims=True), jnp.sum(centere...  23.1 us
    all_gather x2, blocking collectives, forward_tower(): lax.all_gather(row_block, 'tensor', axis=2, tiled=True)  21.3 us
  transfers between devices with their start and end apart: 22, of which 6 were waited for; matrix products, arithmetic and copies ran while one was open for 34% of the time, Pallas kernels for 0%

profile of v1, /device:TPU:0, one launch (start us, length us, event | category | flops | bytes accessed | tf_op | source)
XLA Modules:
  0.0 968.7 jit_solution(3763269037751807765)
XLA Ops:
  19.1 8.7 all_gather.45
  50.3 12.6 %all_gather.48 = bf16[1,512,768]{1,2,0:T(8,128)(2,1)S(1)} all-gather(bf16[1,512,192]{1,2,0:T(8,128)(2,1)S(1)} %copy-done.70), channel_id=1, replica_groups=mesh['dp'=8,'tensor'=4] {'tensor'}, dimensions={2}, use_global_device_ids=true | all-gather | bytes 983040 | tf_op jit(solution)/shard_map/all_gather | solution.py:86
  63.3 6.8 all-gather.2
  77.1 6.7 all-gather.4
  89.1 13.1 %all_gather.54 = bf16[2,197,768]{1,2,0:T(8,128)(2,1)} all-gather(bf16[2,197,192]{1,2,0:T(8,128)(2,1)S(1)} %copy-done.72), channel_id=1, replica_groups=mesh['dp'=8,'tensor'=4] {'tensor'}, dimensions={2}, use_global_device_ids=true | all-gather | bytes 756480 | tf_op jit(solution)/shard_map/all_gather | solution.py:42
  104.3 7.5 all-reduce.8
  163.2 10.4 %all_gather.56 = bf16[1,512,768]{1,2,0:T(8,128)(2,1)} all-gather(bf16[1,512,192]{1,2,0:T(8,128)(2,1)S(1)} %copy-done.71), channel_id=1, replica_groups=mesh['dp'=8,'tensor'=4] {'tensor'}, dimensions={2}, use_global_device_ids=true | all-gather | bytes 983040 | tf_op jit(solution)/shard_map/all_gather | solution.py:42
  173.7 51.0 %all-reduce.19.cloned.1.call-done = (bf16[1,512,768]{2,1,0:T(8,128)(2,1)}, bf16[1,711,768]{2,1,0:T(8,128)(2,1)}, bf16[2,197,768]{1,0,2:T(2,128)(2,1)}) async-done(((bf16[1,512,768]{2,1,0:T(8,128)(2,1)}, bf16[1,711,768]{2,1,0:T(8,128)(2,1)}, bf16[2,197,768]{1,0,2:T(2,128)(2,1)}), (bf16[1,512,768]{2,1,0:T(8,128)(2,1)}, bf16[1,711,768]{2,1,0:T(8,128)(2,1)}, ...) | async-done | bytes 2483728 | tf_op jit(solution)/shard_map/psum | solution.py:121
  227.8 6.4 multiply_convert_fusion.3
  261.3 9.1 multiply_convert_fusion.2
  280.1 6.7 copy.223
  313.7 6.7 copy.217
  343.0 12.4 %all-reduce.7 = (f32[2,197]{1,0:T(2,128)S(1)}, f32[2,197,1]{1,0,2:T(2,128)}, f32[512]{0:T(512)}, f32[1,512,1]{1,2,0:T(1,128)}, f32[711]{0:T(1024)}, /*index=5*/f32[1,711,1]{1,2,0:T(1,128)}) all-reduce(f32[2,197]{1,0:T(2,128)} %get-tuple-element.88, f32[2,197,1]{1,0,2:T(2,128)} %bitcast.536, ...), channel_id=1, replica_groups=mesh['dp'=8,'tensor'=4] {'tensor'}, use_global_device_ids=true, to_apply=%region_28.30 | all-reduce | flops 3234 | bytes 25872 | tf_op jit(solution)/shard_map/psum | solution.py:52
  360.8 8.9 all_gather.55
  398.9 9.1 all_gather.57
  473.4 11.1 %copy.231 = f32[3,768,768]{1,0,2:T(4,128)} copy(f32[3,768,768]{2,1,0:T(8,128)} %pad_maximum_fusion.1) | data formatting | bytes 14155776
  484.4 8.2 copy.246
  502.4 9.8 %copy.227 = f32[3,768,3,192]{3,2,0,1:T(4,128)} copy(f32[3,768,3,192]{1,3,2,0:T(8,128)} %pad_maximum_fusion.2) | data formatting | bytes 10616832
  512.2 11.2 %reshape.1205 = f32[768,1728]{1,0:T(8,128)} reshape(f32[768,3,3,192]{3,2,1,0:T(4,128)} %bitcast.442) | data formatting | bytes 10616832
  544.5 10.7 %all-reduce.6 = (f32[2,197]{1,0:T(2,128)S(1)}, f32[2,197,1]{1,0,2:T(2,128)S(1)}, f32[512]{0:T(512)S(1)}, f32[1,512,1]{1,2,0:T(1,128)S(1)}, f32[711]{0:T(1024)S(1)}, /*index=5*/f32[1,711,1]{1,2,0:T(1,128)S(1)}) all-reduce(f32[2,197]{1,0:T(2,128)S(1)} %get-tuple-element.106, ...), channel_id=1, replica_groups=mesh['dp'=8,'tensor'=4] {'tensor'}, use_global_device_ids=true, to_apply=%region_34.36 | all-reduce | flops 3234 | bytes 25872 | tf_op jit(solution)/shard_map/psum | solution.py:52
  564.2 38.5 %psum.127 = f32[3,12,192]{2,1,0:T(8,128)S(1)} all-reduce(f32[3,12,192]{2,1,0:T(8,128)S(1)} %pad_maximum_fusion.9), channel_id=1, replica_groups=mesh['dp'=8,'tensor'=4] {'dp'}, use_global_device_ids=true, to_apply=%region_85.87 | all-reduce | flops 6912 | bytes 55296 | tf_op jit(solution)/shard_map/psum | solution.py:339
  607.2 112.3 %reduce-scatter.47.cloned.1.call-done = f32[96,2304]{1,0:T(8,128)} async-done(((f32[768,2304]{1,0:T(8,128)}), f32[96,2304]{1,0:T(8,128)}) %reduce-scatter.47.cloned.1.call-update) | async-done | bytes 884752
  722.2 106.9 %reduce-scatter.43.cloned.1.call-done = f32[96,1728]{1,0:T(8,128)} async-done(((f32[768,1728]{1,0:T(8,128)}), f32[96,1728]{1,0:T(8,128)}) %reduce-scatter.43.cloned.1.call-update) | async-done | bytes 663568
  831.9 129.8 %reduce-scatter.29.cloned.1.call-done = f32[3,96,768]{2,1,0:T(8,128)} async-done(((f32[3,768,768]{2,1,0:T(8,128)}), f32[3,96,768]{2,1,0:T(8,128)}) %reduce-scatter.29.cloned.1.call-update) | async-done | bytes 884752 | tf_op jit(solution)/shard_map/reduce_scatter | solution.py:336
  (709 shorter events, 334.6 us)
Async XLA Ops:
  7.2 117.0 %all-reduce.15.cloned.1.call-start = ((), (), s32[]{:S(2)}) async-start(), calls=%async_computation.10 | async-start | bytes 1228800 | tf_op jit(solution)/shard_map/psum | solution.py:121
  8.5 104.7 %copy-start.140 = (bf16[2,192]{1,0:T(2,128)(2,1)}, bf16[2,192]{1,0:T(2,128)(2,1)S(1)}, u32[]{:S(2)}) copy-start(bf16[2,192]{1,0:T(2,128)(2,1)S(1)} %get-tuple-element.208) | copy-start | bytes 2308
  8.5 25.5 %collective-permute-start = (bf16[2,192]{1,0:T(2,128)(2,1)S(1)}, bf16[2,192]{1,0:T(2,128)(2,1)S(1)}, u32[]{:S(2)}, u32[]{:S(2)}) collective-permute-start(bf16[2,192]{1,0:T(2,128)(2,1)S(1)} %get-tuple-element.207), channel_id=1, source_target_pairs={{0,3},{1,0},{2,1},{3,2},{4,7},{5,4},{6,5},{7,6},{8,11},{9,8},{10,9... | collective-permute-start | bytes 2312 | tf_op jit(solution)/shard_map/ppermute | solution.py:17
  34.1 3.6 collective-permute-start.1
  44.9 97.7 %all-gather.10.cloned.1.call-start = ((), (), s32[]{:S(2)}) async-start(), calls=%async_computation.11 | async-start | bytes 1474560 | tf_op jit(solution)/shard_map/all_gather | solution.py:86
  45.0 67.1 %collective-permute-start.2 = (bf16[2,192]{1,0:T(2,128)(2,1)S(1)}, bf16[2,192]{1,0:T(2,128)(2,1)S(1)}, u32[]{:S(2)}, u32[]{:S(2)}) collective-permute-start(bf16[2,192]{1,0:T(2,128)(2,1)S(1)} %get-tuple-element.209), channel_id=1, source_target_pairs={{0,3},{1,0},{2,1},{3,2},{4,7},{5,4},{6,5},{7,6},{8,11},{9,8},{10,9... | collective-permute-start | bytes 2312 | tf_op jit(solution)/shard_map/ppermute | solution.py:17
  45.1 68.2 %collective-permute-start.4 = (bf16[2,192]{1,0:T(2,128)(2,1)S(1)}, bf16[2,192]{1,0:T(2,128)(2,1)S(1)}, u32[]{:S(2)}, u32[]{:S(2)}) collective-permute-start(bf16[2,192]{1,0:T(2,128)(2,1)S(1)} %get-tuple-element.208), channel_id=1, source_target_pairs={{0,3},{1,0},{2,1},{3,2},{4,7},{5,4},{6,5},{7,6},{8,11},{9,8},{10,9... | collective-permute-start | bytes 2312 | tf_op jit(solution)/shard_map/ppermute | solution.py:17
  46.3 178.4 %all-reduce.19.cloned.1.call-start = ((), (), s32[]{:S(2)}) async-start(), calls=%async_computation.25 | async-start | bytes 5332992 | tf_op jit(solution)/shard_map/psum | solution.py:121
  50.3 68.2 %copy-start.133 = (pred[512]{0:T(512)(128)(4,1)}, pred[512]{0:T(512)(128)(4,1)S(1)}, u32[]{:S(2)}) copy-start(pred[512]{0:T(512)(128)(4,1)S(1)} %iota_compare_fusion.1) | copy-start | bytes 1540
  112.1 3.6 collective-permute-start.3
  113.3 10.1 %collective-permute-start.5 = (bf16[2,384]{1,0:T(2,128)(2,1)S(1)}, bf16[2,384]{1,0:T(2,128)(2,1)S(1)}, u32[]{:S(2)}, u32[]{:S(2)}) collective-permute-start(bf16[2,384]{1,0:T(2,128)(2,1)S(1)} %pad_maximum_fusion.12), channel_id=1, source_target_pairs={{0,2},{1,3},{2,0},{3,1},{4,6},{5,7},{6,4},{7,5},{8,10},{9,11},{10,... | collective-permute-start | bytes 4616 | tf_op jit(solution)/shard_map/ppermute | solution.py:17
  161.3 109.0 %all-gather.12.cloned.1.call-start = ((), (), s32[]{:S(2)}) async-start(), calls=%async_computation.12 | async-start | bytes 1474560 | tf_op jit(solution)/shard_map/all_gather | solution.py:42
  161.9 163.9 %reduce-scatter.35.cloned.1.call-start = ((), (), s32[]{:S(2)}) async-start(), calls=%async_computation.17 | async-start | bytes 983040
  248.4 81.1 %reduce-scatter.31.cloned.1.call-start = ((), (), s32[]{:S(2)}) async-start(), calls=%async_computation.15 | async-start | bytes 983040
  261.0 74.7 %reduce-scatter.39.cloned.1.call-start = ((), (), s32[]{:S(2)}) async-start(), calls=%async_computation.19 | async-start | bytes 1474560
  289.7 99.1 %reduce-scatter.33.cloned.1.call-start = ((), (), s32[]{:S(2)}) async-start(), calls=%async_computation.16 | async-start | bytes 1474560
  323.4 104.3 %all-gather.14.cloned.1.call-start = ((), (), s32[]{:S(2)}) async-start(), calls=%async_computation.13 | async-start | bytes 1474560 | tf_op jit(solution)/shard_map/all_gather | solution.py:42
  398.8 137.5 %all-reduce.17.cloned.1.call-start = ((), (), s32[]{:S(2)}) async-start(), calls=%async_computation.24 | async-start | bytes 3145728
  415.6 123.8 %reduce-scatter.37.cloned.1.call-start = ((), (), s32[]{:S(2)}) async-start(), calls=%async_computation.18 | async-start | bytes 983040
  427.5 114.3 %reduce-scatter.41.cloned.1.call-start = ((), (), s32[]{:S(2)}) async-start(), calls=%async_computation.20 | async-start | bytes 1474560
  453.5 151.7 %reduce-scatter.45.cloned.1.call-start = ((), (), s32[]{:S(2)}) async-start(), calls=%async_computation.22 | async-start | bytes 2211840
  464.1 255.4 %reduce-scatter.47.cloned.1.call-start = ((), (), s32[]{:S(2)}) async-start(), calls=%async_computation.23 | async-start | bytes 7962624
  492.7 336.3 %reduce-scatter.43.cloned.1.call-start = ((), (), s32[]{:S(2)}) async-start(), calls=%async_computation.21 | async-start | bytes 6193152
  523.5 438.2 %reduce-scatter.29.cloned.1.call-start = ((), (), s32[]{:S(2)}) async-start(), calls=%async_computation.14 | async-start | bytes 7962624 | tf_op jit(solution)/shard_map/reduce_scatter | solution.py:336
  (210 other events, 1154.8 us)
Sparse Core Ops, SparseCore 0:
  45.1 36.9 all-reduce.14
  83.6 21.1 all-gather.9
  161.5 63.1 all-reduce.18
  226.1 17.4 all-gather.11
  248.5 23.3 reduce-scatter.34
  274.3 23.2 reduce-scatter.30
  300.1 25.5 reduce-scatter.38
  328.3 25.7 reduce-scatter.32
  398.9 17.5 all-gather.13
  419.9 42.8 all-reduce.16
  465.4 23.2 reduce-scatter.36
  491.1 25.6 reduce-scatter.40
  520.2 67.6 reduce-scatter.44
  591.4 128.0 reduce-scatter.46
  723.0 106.0 reduce-scatter.42
  833.2 128.5 reduce-scatter.28
